TPU v7x, 128 devices: a whole 4x4x4 slice. The times are simulated.
128 devices in a mesh: pb: 8 (over x, core), kv: 8 (over z_lo, y), ha: 2 (over z_hi).
Axes of the slice: x: 4, y: 4, z: 4 (z_hi: 2, z_lo: 2; z = z_hi * 2 + z_lo), core: 2. Of those that a mesh axis runs over, the one named last changes fastest.
Arguments:
- queries: bfloat16 [12288, 2048], P(('pb', 'kv', 'ha')), may hold values from -48 to 48
- keys: bfloat16 [12288, 2048], P(('pb', 'kv', 'ha')), may hold values from -6 to 6
- values: bfloat16 [12288, 2048], P(('pb', 'kv', 'ha')), may hold values from -6 to 6
- masked_at: int32 [3072], replicated, may hold values from 0 to 12287, as said below
- mask_query: bfloat16 [2048], replicated, may hold values from -6 to 6
- mask_key: bfloat16 [2048], replicated, may hold values from -6 to 6
- mask_value: bfloat16 [2048], replicated, may hold values from -6 to 6
Outputs:
- attended: bfloat16 [12288, 2048], P(('pb', 'kv', 'ha'))
Inputs may be any that keep to these rules, and one draw needn't show every extreme that they name: `masked_at`: 3072 distinct positions in rising order.
All inputs are finite; a program needn't handle non-finite values.
Results may differ from a plain program's by a relative error of at most 0.006.
Values may be sent and summed in bfloat16 or wider, within the bound.
No kernel may reach another device: no remote copies, remote signals or barrier semaphores. Data moves between devices by JAX's collectives and lax.ppermute only.
A program may use at most 128 MiB of HBM per device.

v0:
```python
import math
import jax
import jax.numpy as jnp
from jax import lax
from jax.sharding import PartitionSpec as P

DH = 128
HEADS = 16
rope_theta = 500000.0
very_negative = -1e30


def side_by_side(arrays, axis, dim, along):
    both = jnp.concatenate(arrays, axis=along)
    whole, at, gathered = (lax.all_gather(both, axis, axis=dim, tiled=True), 0, [])
    for a in arrays:
        gathered.append(lax.slice_in_dim(whole, at, at + a.shape[along], axis=along))
        at += a.shape[along]
    return tuple(gathered)


def rotated(vector, positions):
    halves = DH // 2
    exponent = jnp.arange(halves, dtype=jnp.float32) * (2.0 / DH)
    inverse = 1.0 / rope_theta**exponent
    angles = positions.astype(jnp.float32)[:, None] * inverse[None, :]
    cosine = jnp.cos(angles)[:, None, :]
    sine_part = jnp.sin(angles)[:, None, :]
    per_head = vector.astype(jnp.float32).reshape(HEADS, DH)
    first_half = per_head[None, :, :halves]
    second = per_head[None, :, halves:]
    result = jnp.concatenate(
        [first_half * cosine - second * sine_part, second * cosine + first_half * sine_part], axis=2
    )
    return result.reshape(positions.shape[0], HEADS * DH).astype(jnp.bfloat16)


def attend_piece(running, head_queries, piece_keys, piece_values, score_scale):
    head_total = head_queries.shape[0]

    def per_head(packed):
        head_index, query_part, old_max, old_total, old_sum = packed
        key_part = lax.dynamic_slice_in_dim(piece_keys, head_index * DH, DH, 1)
        value_part = lax.dynamic_slice_in_dim(piece_values, head_index * DH, DH, 1)
        scores = (
            jnp.einsum("qd,kd->qk", query_part, key_part, preferred_element_type=jnp.float32)
            * score_scale
        )
        new_max = jnp.maximum(old_max, jnp.max(scores, axis=1))
        factor = jnp.exp(old_max - new_max)
        weights = jnp.exp(scores - new_max[:, None])
        new_total = old_total * factor + jnp.sum(weights, axis=1)
        new_sum = old_sum * factor[:, None] + jnp.dot(
            weights.astype(jnp.bfloat16), value_part, preferred_element_type=jnp.float32
        )
        return (new_max, new_total, new_sum)

    return lax.map(
        per_head,
        (jnp.arange(head_total, dtype=jnp.int32), head_queries, running[0], running[1], running[2]),
    )


def finish(received):
    part_max, part_total, part_sum = received
    joint_max = jnp.max(part_max, axis=0)
    factor = jnp.exp(part_max - joint_max[None])
    total_sum = jnp.sum(part_total * factor, axis=0)
    summed = jnp.sum(part_sum * factor[..., None], axis=0)
    return summed / total_sum[..., None]


def starting(head_total, query_total):
    return (
        jnp.full((head_total, query_total), very_negative, jnp.float32),
        jnp.zeros((head_total, query_total), jnp.float32),
        jnp.zeros((head_total, query_total, DH), jnp.float32),
    )


def body(queries, keys, values, masked_at, mask_query, mask_key, mask_value):
    local_rows = queries.shape[0]
    full_width = queries.shape[1]
    first_row = lax.axis_index(("pb", "kv", "ha")) * local_rows
    positions = first_row + jnp.arange(local_rows, dtype=jnp.int32)
    masked_flags = jnp.any(positions[:, None] == masked_at[None, :], axis=1)
    query_used = jnp.where(masked_flags[:, None], rotated(mask_query, positions), queries)
    key_used = jnp.where(masked_flags[:, None], rotated(mask_key, positions), keys)
    value_used = jnp.where(masked_flags[:, None], mask_value[None, :], values)
    group_width = full_width // lax.axis_size("ha")
    head_total = group_width // DH
    score_scale = 1.0 / math.sqrt(DH)
    query_group, key_group, value_group = (
        lax.all_to_all(query_used, "ha", split_axis=1, concat_axis=0, tiled=True),
        lax.all_to_all(key_used, "ha", split_axis=1, concat_axis=0, tiled=True),
        lax.all_to_all(value_used, "ha", split_axis=1, concat_axis=0, tiled=True),
    )
    own_queries = lax.all_gather(query_group, "kv", axis=0, tiled=True)
    query_total = own_queries.shape[0]
    head_queries = own_queries.reshape(query_total, head_total, DH).transpose(1, 0, 2)
    portion = side_by_side((key_group, value_group), "pb", 0, 1)
    running = attend_piece(
        starting(head_total, query_total), head_queries, portion[0], portion[1], score_scale
    )
    owned_rows = query_total // lax.axis_size("kv")
    stacked = (running[0][None], running[1][None], running[2][None])
    normalized = finish(
        (
            lax.all_to_all(stacked[0], "kv", split_axis=2, concat_axis=0, tiled=True),
            lax.all_to_all(stacked[1], "kv", split_axis=2, concat_axis=0, tiled=True),
            lax.all_to_all(stacked[2], "kv", split_axis=2, concat_axis=0, tiled=True),
        )
    )
    out_rows = normalized.transpose(1, 0, 2).reshape(owned_rows, group_width).astype(jnp.bfloat16)
    return lax.all_to_all(out_rows, "ha", split_axis=0, concat_axis=1, tiled=True)


def solution(mesh):
    in_specs = (
        P(("pb", "kv", "ha"), None),
        P(("pb", "kv", "ha"), None),
        P(("pb", "kv", "ha"), None),
        P(),
        P(),
        P(),
        P(),
    )
    out_specs = P(("pb", "kv", "ha"), None)
    return jax.shard_map(body, mesh=mesh, in_specs=in_specs, out_specs=out_specs, check_vma=False)
```

profile of v0, /device:TPU:24, one launch (start us, length us, event | category | flops | bytes accessed | tf_op | source)
XLA Modules:
  0.0 589.7 jit_solution(16703127739279018998)
XLA Ops:
  11.7 13.1 %all_to_all.127 = bf16[96,2,1024]{2,0,1:T(8,128)(2,1)} all-to-all(bf16[96,2,1024]{2,0,1:T(8,128)(2,1)S(1)} %bitcast.98), channel_id=1, replica_groups=mesh['pb'=8,'kv'=8,'ha'=2] {'ha'}, dimensions={1} | all-to-all | bytes 786432 | tf_op jit(solution)/shard_map/all_to_all | solution.py:94
  29.2 11.5 %all-to-all-done.2 = bf16[96,2,1024]{2,0,1:T(8,128)(2,1)S(1)} async-done(((bf16[96,2,1024]{2,0,1:T(8,128)(2,1)}), bf16[96,2,1024]{2,0,1:T(8,128)(2,1)S(1)}, u32[]{:S(2)}, u32[]{:S(2)}) %all-to-all-start.2) | async-done | bytes 393248 | tf_op jit(solution)/shard_map/all_to_all | solution.py:96
  40.7 29.5 %all_to_all.128 = bf16[96,2,1024]{2,0,1:T(8,128)(2,1)S(1)} all-to-all(bf16[96,2,1024]{2,0,1:T(8,128)(2,1)S(1)} %bitcast.97), channel_id=1, replica_groups=mesh['pb'=8,'kv'=8,'ha'=2] {'ha'}, dimensions={1} | all-to-all | bytes 786432 | tf_op jit(solution)/shard_map/all_to_all | solution.py:95
  76.0 35.1 %all-gather.5.cloned.1.call-done = bf16[1536,2048]{1,0:T(8,128)(2,1)} async-done(((bf16[192,2048]{1,0:T(8,128)(2,1)}), bf16[1536,2048]{1,0:T(8,128)(2,1)}) %all-gather.5.cloned.1.call-update) | async-done | bytes 6291472 | tf_op jit(solution)/shard_map/all_gather | solution.py:15
  111.0 6.1 %fusion.21 = (bf16[1536,1024]{1,0:T(8,128)(2,1)}, bf16[1536,1024]{1,0:T(8,128)(2,1)}) fusion(bf16[1536,2048]{1,0:T(8,128)(2,1)} %all-gather.5.cloned.1.call-done), kind=kLoop, calls=%fused_computation.47 | loop fusion | bytes 12582912 | tf_op jit(solution)/shard_map/slice | solution.py:17
  117.2 319.7 %while.14 = (s32[]{:T(128)}, f32[8,1536]{1,0:T(8,128)S(1)}, f32[8,1536]{1,0:T(8,128)S(1)}, f32[8,1536,128]{2,0,1:T(8,128)}, bf16[8,1536,128]{1,2,0:T(8,128)(2,1)...) while((s32[]{:T(128)}, f32[8,1536]{1,0:T(8,128)S(1)}, ...), condition=%wide.region_4.5_spmd, body=%wide.region_1.4_spmd.sunk | while | flops 1222318080 | bytes 31955152 | solution.py:58
  118.6 6.1 %fusion.31 = (f32[1536]{0:T(1024)S(1)}, f32[1536,1536]{0,1:T(8,128)}) fusion(bf16[8,1536,128]{1,2,0:T(8,128)(2,1)} %get-tuple-element.212, s32[]{:T(128)S(6)} %copy.73, bf16[1536,1024]{1,0:T(8,128)(2,1)} %get-tuple-element.214, s32[]{:T(128)S(6)} %select_n.22), kind=kOutput, calls=%fused_computation.46.clone.1 | convolution fusion | flops 608696832 | bytes 10229768 | tf_op jit(solution)/shard_map/while/body/eval_jaxpr/qd,kd->qk/dot_general | solution.py:46
  135.6 21.6 %dynamic_update_slice.16 = f32[8,1536,128]{2,0,1:T(8,128)} dynamic-update-slice(f32[8,1536,128]{2,0,1:T(8,128)} %get-tuple-element.199, f32[1,1536,128]{2,0,1:T(1,128)S(1)} %bitcast.90, s32[]{:T(128)S(6)} %copy.73, s32[]{:T(128)} %constant.30.clone.1..sunk, s32[]{:T(128)} %constant.30.clone.1..sunk) | dynamic-update-slice | bytes 1572868 | tf_op jit(solution)/shard_map/while/body/jit(dynamic_update_index_in_dim)/dynamic_update_slice | solution.py:58
  158.5 6.1 %fusion.31 = (f32[1536]{0:T(1024)S(1)}, f32[1536,1536]{0,1:T(8,128)}) fusion(bf16[8,1536,128]{1,2,0:T(8,128)(2,1)} %get-tuple-element.212, s32[]{:T(128)S(6)} %copy.73, bf16[1536,1024]{1,0:T(8,128)(2,1)} %get-tuple-element.214, s32[]{:T(128)S(6)} %select_n.22), kind=kOutput, calls=%fused_computation.46.clone.1 | convolution fusion | flops 608696832 | bytes 10229768 | tf_op jit(solution)/shard_map/while/body/eval_jaxpr/qd,kd->qk/dot_general | solution.py:46
  170.0 5.5 fusion.33
  175.5 21.6 %dynamic_update_slice.16 = f32[8,1536,128]{2,0,1:T(8,128)} dynamic-update-slice(f32[8,1536,128]{2,0,1:T(8,128)} %get-tuple-element.199, f32[1,1536,128]{2,0,1:T(1,128)S(1)} %bitcast.90, s32[]{:T(128)S(6)} %copy.73, s32[]{:T(128)} %constant.30.clone.1..sunk, s32[]{:T(128)} %constant.30.clone.1..sunk) | dynamic-update-slice | bytes 1572868 | tf_op jit(solution)/shard_map/while/body/jit(dynamic_update_index_in_dim)/dynamic_update_slice | solution.py:58
  198.5 6.1 %fusion.31 = (f32[1536]{0:T(1024)S(1)}, f32[1536,1536]{0,1:T(8,128)}) fusion(bf16[8,1536,128]{1,2,0:T(8,128)(2,1)} %get-tuple-element.212, s32[]{:T(128)S(6)} %copy.73, bf16[1536,1024]{1,0:T(8,128)(2,1)} %get-tuple-element.214, s32[]{:T(128)S(6)} %select_n.22), kind=kOutput, calls=%fused_computation.46.clone.1 | convolution fusion | flops 608696832 | bytes 10229768 | tf_op jit(solution)/shard_map/while/body/eval_jaxpr/qd,kd->qk/dot_general | solution.py:46
  210.0 5.5 fusion.33
  215.5 21.6 %dynamic_update_slice.16 = f32[8,1536,128]{2,0,1:T(8,128)} dynamic-update-slice(f32[8,1536,128]{2,0,1:T(8,128)} %get-tuple-element.199, f32[1,1536,128]{2,0,1:T(1,128)S(1)} %bitcast.90, s32[]{:T(128)S(6)} %copy.73, s32[]{:T(128)} %constant.30.clone.1..sunk, s32[]{:T(128)} %constant.30.clone.1..sunk) | dynamic-update-slice | bytes 1572868 | tf_op jit(solution)/shard_map/while/body/jit(dynamic_update_index_in_dim)/dynamic_update_slice | solution.py:58
  238.5 6.1 %fusion.31 = (f32[1536]{0:T(1024)S(1)}, f32[1536,1536]{0,1:T(8,128)}) fusion(bf16[8,1536,128]{1,2,0:T(8,128)(2,1)} %get-tuple-element.212, s32[]{:T(128)S(6)} %copy.73, bf16[1536,1024]{1,0:T(8,128)(2,1)} %get-tuple-element.214, s32[]{:T(128)S(6)} %select_n.22), kind=kOutput, calls=%fused_computation.46.clone.1 | convolution fusion | flops 608696832 | bytes 10229768 | tf_op jit(solution)/shard_map/while/body/eval_jaxpr/qd,kd->qk/dot_general | solution.py:46
  255.5 21.6 %dynamic_update_slice.16 = f32[8,1536,128]{2,0,1:T(8,128)} dynamic-update-slice(f32[8,1536,128]{2,0,1:T(8,128)} %get-tuple-element.199, f32[1,1536,128]{2,0,1:T(1,128)S(1)} %bitcast.90, s32[]{:T(128)S(6)} %copy.73, s32[]{:T(128)} %constant.30.clone.1..sunk, s32[]{:T(128)} %constant.30.clone.1..sunk) | dynamic-update-slice | bytes 1572868 | tf_op jit(solution)/shard_map/while/body/jit(dynamic_update_index_in_dim)/dynamic_update_slice | solution.py:58
  278.4 6.1 %fusion.31 = (f32[1536]{0:T(1024)S(1)}, f32[1536,1536]{0,1:T(8,128)}) fusion(bf16[8,1536,128]{1,2,0:T(8,128)(2,1)} %get-tuple-element.212, s32[]{:T(128)S(6)} %copy.73, bf16[1536,1024]{1,0:T(8,128)(2,1)} %get-tuple-element.214, s32[]{:T(128)S(6)} %select_n.22), kind=kOutput, calls=%fused_computation.46.clone.1 | convolution fusion | flops 608696832 | bytes 10229768 | tf_op jit(solution)/shard_map/while/body/eval_jaxpr/qd,kd->qk/dot_general | solution.py:46
  295.4 21.6 %dynamic_update_slice.16 = f32[8,1536,128]{2,0,1:T(8,128)} dynamic-update-slice(f32[8,1536,128]{2,0,1:T(8,128)} %get-tuple-element.199, f32[1,1536,128]{2,0,1:T(1,128)S(1)} %bitcast.90, s32[]{:T(128)S(6)} %copy.73, s32[]{:T(128)} %constant.30.clone.1..sunk, s32[]{:T(128)} %constant.30.clone.1..sunk) | dynamic-update-slice | bytes 1572868 | tf_op jit(solution)/shard_map/while/body/jit(dynamic_update_index_in_dim)/dynamic_update_slice | solution.py:58
  318.4 6.1 %fusion.31 = (f32[1536]{0:T(1024)S(1)}, f32[1536,1536]{0,1:T(8,128)}) fusion(bf16[8,1536,128]{1,2,0:T(8,128)(2,1)} %get-tuple-element.212, s32[]{:T(128)S(6)} %copy.73, bf16[1536,1024]{1,0:T(8,128)(2,1)} %get-tuple-element.214, s32[]{:T(128)S(6)} %select_n.22), kind=kOutput, calls=%fused_computation.46.clone.1 | convolution fusion | flops 608696832 | bytes 10229768 | tf_op jit(solution)/shard_map/while/body/eval_jaxpr/qd,kd->qk/dot_general | solution.py:46
  329.9 5.6 fusion.33
  335.4 21.6 %dynamic_update_slice.16 = f32[8,1536,128]{2,0,1:T(8,128)} dynamic-update-slice(f32[8,1536,128]{2,0,1:T(8,128)} %get-tuple-element.199, f32[1,1536,128]{2,0,1:T(1,128)S(1)} %bitcast.90, s32[]{:T(128)S(6)} %copy.73, s32[]{:T(128)} %constant.30.clone.1..sunk, s32[]{:T(128)} %constant.30.clone.1..sunk) | dynamic-update-slice | bytes 1572868 | tf_op jit(solution)/shard_map/while/body/jit(dynamic_update_index_in_dim)/dynamic_update_slice | solution.py:58
  358.4 6.1 %fusion.31 = (f32[1536]{0:T(1024)S(1)}, f32[1536,1536]{0,1:T(8,128)}) fusion(bf16[8,1536,128]{1,2,0:T(8,128)(2,1)} %get-tuple-element.212, s32[]{:T(128)S(6)} %copy.73, bf16[1536,1024]{1,0:T(8,128)(2,1)} %get-tuple-element.214, s32[]{:T(128)S(6)} %select_n.22), kind=kOutput, calls=%fused_computation.46.clone.1 | convolution fusion | flops 608696832 | bytes 10229768 | tf_op jit(solution)/shard_map/while/body/eval_jaxpr/qd,kd->qk/dot_general | solution.py:46
  375.4 21.6 %dynamic_update_slice.16 = f32[8,1536,128]{2,0,1:T(8,128)} dynamic-update-slice(f32[8,1536,128]{2,0,1:T(8,128)} %get-tuple-element.199, f32[1,1536,128]{2,0,1:T(1,128)S(1)} %bitcast.90, s32[]{:T(128)S(6)} %copy.73, s32[]{:T(128)} %constant.30.clone.1..sunk, s32[]{:T(128)} %constant.30.clone.1..sunk) | dynamic-update-slice | bytes 1572868 | tf_op jit(solution)/shard_map/while/body/jit(dynamic_update_index_in_dim)/dynamic_update_slice | solution.py:58
  398.3 6.1 %fusion.31 = (f32[1536]{0:T(1024)S(1)}, f32[1536,1536]{0,1:T(8,128)}) fusion(bf16[8,1536,128]{1,2,0:T(8,128)(2,1)} %get-tuple-element.212, s32[]{:T(128)S(6)} %copy.73, bf16[1536,1024]{1,0:T(8,128)(2,1)} %get-tuple-element.214, s32[]{:T(128)S(6)} %select_n.22), kind=kOutput, calls=%fused_computation.46.clone.1 | convolution fusion | flops 608696832 | bytes 10229768 | tf_op jit(solution)/shard_map/while/body/eval_jaxpr/qd,kd->qk/dot_general | solution.py:46
  415.3 21.6 %dynamic_update_slice.16 = f32[8,1536,128]{2,0,1:T(8,128)} dynamic-update-slice(f32[8,1536,128]{2,0,1:T(8,128)} %get-tuple-element.199, f32[1,1536,128]{2,0,1:T(1,128)S(1)} %bitcast.90, s32[]{:T(128)S(6)} %copy.73, s32[]{:T(128)} %constant.30.clone.1..sunk, s32[]{:T(128)} %constant.30.clone.1..sunk) | dynamic-update-slice | bytes 1572868 | tf_op jit(solution)/shard_map/while/body/jit(dynamic_update_index_in_dim)/dynamic_update_slice | solution.py:58
  437.7 7.1 %reduce.1 = f32[1536,8]{1,0:T(8,128)S(1)} reduce(f32[1536,1,8]{2,1,0:T(1,128)S(1)} %bitcast.92, f32[]{:T(128)} %broadcast.133), dimensions={1}, to_apply=%bitcast.76.reduce_sub_computation | reduce | bytes 98308
  445.8 5.8 all-to-all-start.5
  451.9 7.1 %reduce.3 = f32[1536,8]{1,0:T(8,128)S(1)} reduce(f32[1536,1,8]{2,1,0:T(1,128)S(1)} %bitcast.93, f32[]{:T(128)} %broadcast.133), dimensions={1}, to_apply=%bitcast.74.reduce_sub_computation | reduce | bytes 98308
  459.4 9.8 %all_to_all.129 = f32[8,1,1536]{2,1,0:T(1,128)S(1)} all-to-all(f32[8,1,1536]{2,1,0:T(1,128)S(1)} %reshape.156), channel_id=1, replica_groups=mesh['pb'=8,'kv'=8,'ha'=2] {'kv'}, dimensions={0} | all-to-all | bytes 98304 | tf_op jit(solution)/shard_map/all_to_all | solution.py:109
  469.2 6.6 %all-to-all-start.3 = ((f32[1,8,1536,128]{3,1,0,2:T(8,128)}), f32[1,8,1536,128]{3,1,0,2:T(8,128)}, u32[]{:S(2)}, u32[]{:S(2)}) async-start(f32[1,8,1536,128]{3,1,0,2:T(8,128)} %bitcast.91), calls=%async_computation.3 | async-start | bytes 12582912 | tf_op jit(solution)/shard_map/all_to_all | solution.py:111
  480.4 84.7 %all-to-all-done.3 = f32[1,8,1536,128]{3,1,0,2:T(8,128)} async-done(((f32[1,8,1536,128]{3,1,0,2:T(8,128)}), f32[1,8,1536,128]{3,1,0,2:T(8,128)}, u32[]{:S(2)}, u32[]{:S(2)}) %all-to-all-start.3) | async-done | bytes 6291488 | tf_op jit(solution)/shard_map/all_to_all | solution.py:111
  570.8 11.4 %all_to_all.130 = bf16[2,96,1024]{2,1,0:T(8,128)(2,1)S(1)} all-to-all(bf16[2,96,1024]{2,1,0:T(8,128)(2,1)S(1)} %convert_element_type.32), channel_id=1, replica_groups=mesh['pb'=8,'kv'=8,'ha'=2] {'ha'}, dimensions={0} | all-to-all | bytes 786432 | tf_op jit(solution)/shard_map/all_to_all | solution.py:115
  (106 shorter events, 104.1 us)
Async XLA Ops:
  6.5 64.7 %all-gather.3.cloned.1.call-start = ((), (), s32[]{:S(2)}) async-start(), calls=%async_computation.7 | async-start | bytes 3538944 | tf_op jit(solution)/shard_map/all_gather | solution.py:98
  25.6 15.1 %all-to-all-start.2 = ((bf16[96,2,1024]{2,0,1:T(8,128)(2,1)}), bf16[96,2,1024]{2,0,1:T(8,128)(2,1)S(1)}, u32[]{:S(2)}, u32[]{:S(2)}) async-start(bf16[96,2,1024]{2,0,1:T(8,128)(2,1)} %bitcast.81), calls=%async_computation.2 | async-start | bytes 786432 | tf_op jit(solution)/shard_map/all_to_all | solution.py:96
  29.1 81.9 %all-gather.5.cloned.1.call-start = ((), (), s32[]{:S(2)}) async-start(), calls=%async_computation.8 | async-start | bytes 7077888 | tf_op jit(solution)/shard_map/all_gather | solution.py:15
  445.8 13.6 %all-to-all-start.5 = ((f32[8,1,1536]{2,1,0:T(1,128)}), f32[8,1,1536]{2,1,0:T(1,128)S(1)}, u32[]{:S(2)}, u32[]{:S(2)}) async-start(f32[8,1,1536]{2,1,0:T(1,128)} %reshape.158), calls=%async_computation.5 | async-start | bytes 98304 | tf_op jit(solution)/shard_map/all_to_all | solution.py:110
  469.2 95.9 %all-to-all-start.3 = ((f32[1,8,1536,128]{3,1,0,2:T(8,128)}), f32[1,8,1536,128]{3,1,0,2:T(8,128)}, u32[]{:S(2)}, u32[]{:S(2)}) async-start(f32[1,8,1536,128]{3,1,0,2:T(8,128)} %bitcast.91), calls=%async_computation.3 | async-start | bytes 12582912 | tf_op jit(solution)/shard_map/all_to_all | solution.py:111
Sparse Core Ops, SparseCore 0:
  25.0 41.8 all-gather.2
  71.3 39.6 all-gather.4
where the time goes:
time: 595 us; the launch traced here: 590 us
  local copies, waits for them, and re-layouts  199 us (33%)
  waiting for transfers between devices  131 us (22%)
  matrix products  93.2 us (16%)
  other arithmetic  67 us (11%)
  blocking collectives  63.8 us (11%)
  starting transfers between devices  15.9 us (3%)
  between operations  13.6 us (2%)
    dynamic_update_slice x24, local copies, waits for them, and re-layouts, attend_piece(): lax.map(per_head, (jnp.arange(head_total, dtype=jnp.int32), head_queries,...  175 us
    all_to_all x1, waiting for transfers between devices, body(): lax.all_to_all(stacked[2], 'kv', split_axis=2, concat_axis=0, tiled=True)  84.7 us
    dot_general x8, matrix products, per_head(): jnp.einsum('qd,kd->qk', query_part, key_part, preferred_element_type=jnp....  49.1 us
    dot_general x8, matrix products, per_head(): jnp.dot(weights.astype(jnp.bfloat16), value_part, preferred_element_type=...  44.2 us
    reduce_sum x8, other arithmetic, per_head(): new_total = old_total * factor + jnp.sum(weights, axis=1)  39.9 us
    all_gather x1, waiting for transfers between devices, side_by_side(): lax.all_gather(both, axis, axis=dim, tiled=True)  35.1 us
    all_to_all x1, blocking collectives, body(): lax.all_to_all(key_used, 'ha', split_axis=1, concat_axis=0, tiled=True)  29.5 us
    unnamed x2, other arithmetic  14.2 us
  transfers between devices with their start and end apart: 5, of which 3 were waited for; matrix products, arithmetic and copies ran while one was open for 3% of the time, Pallas kernels for 0%

commit v1 on v0

--- a/solution.py
+++ b/solution.py
@@ -1,3 +1,4 @@
+import functools
 import math
 import jax
 import jax.numpy as jnp
@@ -8,6 +9,21 @@
 HEADS = 16
 rope_theta = 500000.0
 very_negative = -1e30
+
+
+def shape_side(patch, a_name):
+    return jnp.concatenate(
+        lax.all_to_all(
+            jnp.stack(jnp.split(patch, lax.axis_size(a_name), 2), 0),
+            axis_name=a_name,
+            split_axis=0,
+            concat_axis=0,
+        ),
+        0,
+    )
+
+
+desk_trace = functools.partial(shape_side, a_name="kv")
 
 
 def side_by_side(arrays, axis, dim, along):
@@ -108,7 +124,7 @@
         (
             lax.all_to_all(stacked[0], "kv", split_axis=2, concat_axis=0, tiled=True),
             lax.all_to_all(stacked[1], "kv", split_axis=2, concat_axis=0, tiled=True),
-            lax.all_to_all(stacked[2], "kv", split_axis=2, concat_axis=0, tiled=True),
+            desk_trace(stacked[2]),
         )
     )
     out_rows = normalized.transpose(1, 0, 2).reshape(owned_rows, group_width).astype(jnp.bfloat16)

time: 595 us -> 361 us (0.61)
  local copies, waits for them, and re-layouts: 199 us -> 41.7 us
  matrix products: 93.2 us -> 50.2 us
  other arithmetic: 67 us -> 37.7 us
  blocking collectives: 63.8 us -> 53.9 us
    dynamic_update_slice x24 -> x16, local copies, waits for them, and re-layouts: 175 us -> 2.52 us  [attend_piece(): lax.map(per_head, (jnp.arange(head_total, dtype=jnp.int32), head_queries,...]
    dot_general x8, matrix products: 49.1 us -> 19.1 us  [per_head(): jnp.einsum('qd,kd->qk', query_part, key_part, preferred_element_type=jnp....]
    reduce_sum x8, other arithmetic: 39.9 us -> 10.6 us  [per_head(): new_total = old_total * factor + jnp.sum(weights, axis=1)]
    unnamed x5 -> x12, local copies, waits for them, and re-layouts: 4.4 us -> 19.8 us
    dot_general x8, matrix products: 44.2 us -> 31.1 us  [per_head(): jnp.dot(weights.astype(jnp.bfloat16), value_part, preferred_element_type=...]
    all_to_all x2 -> x1, blocking collectives: 39.3 us -> 29.5 us  [body(): lax.all_to_all(value_used, 'ha', split_axis=1, concat_axis=0, tiled=True)]
    all_to_all x2 -> x3, starting transfers between devices: 10.1 us -> 15.9 us  [the longest x1 6.63 us: shape_side(): lax.all_to_all(jnp.stack(jnp.split(patch, lax.axis_size(a_name), 2), 0),...]
    all_to_all x2 -> x3, waiting for transfers between devices: 96.2 us -> 96.2 us  [the longest x1 84.7 us: shape_side(): lax.all_to_all(jnp.stack(jnp.split(patch, lax.axis_size(a_name), 2), 0),...]
  transfers between devices with their start and end apart: 5 -> 6, of which waited for: 3 -> 4; matrix products, arithmetic and copies ran while one was open for 3% -> 10% of each run, Pallas kernels for 0% -> 0%
where the time goes in v1:
time: 361 us; the launch traced here: 359 us
  waiting for transfers between devices  135 us (37%)
  blocking collectives  53.9 us (15%)
  matrix products  50.2 us (14%)
  local copies, waits for them, and re-layouts  41.7 us (12%)
  other arithmetic  37.7 us (10%)
  starting transfers between devices  21.6 us (6%)
  between operations  13.6 us (4%)
  loops' own time  5.11 us (1%)
    all_to_all x1, waiting for transfers between devices, shape_side(): lax.all_to_all(jnp.stack(jnp.split(patch, lax.axis_size(a_name), 2), 0),...  84.7 us
    all_gather x1, waiting for transfers between devices, side_by_side(): lax.all_gather(both, axis, axis=dim, tiled=True)  36.6 us
    dot_general x8, matrix products, per_head(): jnp.dot(weights.astype(jnp.bfloat16), value_part, preferred_element_type=...  31.1 us
    all_to_all x1, blocking collectives, body(): lax.all_to_all(value_used, 'ha', split_axis=1, concat_axis=0, tiled=True)  29.5 us
    unnamed x12, local copies, waits for them, and re-layouts  19.8 us
    dot_general x8, matrix products, per_head(): jnp.einsum('qd,kd->qk', query_part, key_part, preferred_element_type=jnp....  19.1 us
    unnamed x2, other arithmetic  14.4 us
    all_to_all x1, blocking collectives, body(): lax.all_to_all(query_used, 'ha', split_axis=1, concat_axis=0, tiled=True)  13.1 us
  transfers between devices with their start and end apart: 6, of which 4 were waited for; matrix products, arithmetic and copies ran while one was open for 10% of the time, Pallas kernels for 0%

profile of v1, /device:TPU:24, one launch (start us, length us, event | category | flops | bytes accessed | tf_op | source)
XLA Modules:
  0.0 358.9 jit_solution(6360371607480611116)
XLA Ops:
  11.7 13.1 %all_to_all.114 = bf16[96,2,1024]{2,0,1:T(8,128)(2,1)} all-to-all(bf16[96,2,1024]{2,0,1:T(8,128)(2,1)S(1)} %bitcast.127), channel_id=1, replica_groups=mesh['pb'=8,'kv'=8,'ha'=2] {'ha'}, dimensions={1} | all-to-all | bytes 786432 | tf_op jit(solution)/shard_map/all_to_all | solution.py:110
  25.6 3.5 all-to-all-start.1
  29.2 11.5 %all-to-all-done.1 = bf16[96,2,1024]{2,0,1:T(8,128)(2,1)S(1)} async-done(((bf16[96,2,1024]{2,0,1:T(8,128)(2,1)}), bf16[96,2,1024]{2,0,1:T(8,128)(2,1)S(1)}, u32[]{:S(2)}, u32[]{:S(2)}) %all-to-all-start.1) | async-done | bytes 393248 | tf_op jit(solution)/shard_map/all_to_all | solution.py:111
  40.7 29.5 %all_to_all.115 = bf16[96,2,1024]{2,0,1:T(8,128)(2,1)S(1)} all-to-all(bf16[96,2,1024]{2,0,1:T(8,128)(2,1)S(1)} %bitcast.126), channel_id=1, replica_groups=mesh['pb'=8,'kv'=8,'ha'=2] {'ha'}, dimensions={1} | all-to-all | bytes 786432 | tf_op jit(solution)/shard_map/all_to_all | solution.py:112
  71.3 3.2 copy.38
  74.5 36.6 %all-gather.5.cloned.1.call-done = bf16[1536,2048]{1,0:T(8,128)(2,1)} async-done(((bf16[192,2048]{1,0:T(8,128)(2,1)}), bf16[1536,2048]{1,0:T(8,128)(2,1)}) %all-gather.5.cloned.1.call-update) | async-done | bytes 6291472 | tf_op jit(solution)/shard_map/all_gather | solution.py:31
  111.1 6.2 %fusion.35 = (bf16[1536,1024]{1,0:T(8,128)(2,1)}, bf16[1536,1024]{1,0:T(8,128)(2,1)}) fusion(bf16[1536,2048]{1,0:T(8,128)(2,1)} %all-gather.5.cloned.1.call-done), kind=kLoop, calls=%fused_computation.65 | loop fusion | bytes 12582912 | tf_op jit(solution)/shard_map/slice | solution.py:33
  117.2 73.4 %while.14 = (s32[]{:T(128)}, f32[8,1536]{1,0:T(8,128)S(1)}, f32[8,1536]{1,0:T(8,128)S(1)}, f32[8,1536,128]{2,1,0:T(8,128)}, bf16[8,1536,128]{1,2,0:T(8,128)(2,1)...) while((s32[]{:T(128)}, f32[8,1536]{1,0:T(8,128)S(1)}, ...), condition=%wide.region_4.5_spmd, body=%wide.region_1.4_spmd.sunk | while | flops 1222318080 | bytes 30383296 | solution.py:74
  118.4 2.4 fusion.45
  120.8 3.9 %fusion.47 = f32[8,1536,128]{2,1,0:T(8,128)} fusion(f32[8,1536,128]{2,1,0:T(8,128)} %get-tuple-element.199, s32[]{:T(128)} %get-tuple-element.196, f32[1536,1536]{0,1:T(8,128)S(1)} %get-tuple-element.182, f32[1536]{0:T(1024)S(1)} %get-tuple-element.181, bf16[1536,1024]{1,0:T(8,128)(2,1)} %get-tuple-element.215, s32[]{:T(128)S(6)} %select_n.22, ...), kind=kOutput, calls=%fused_computation.8.clone.1 | convolution fusion | flops 608894976 | bytes 10629636 | tf_op jit(solution)/shard_map/while/body/eval_jaxpr/dot_general | solution.py:69
  127.6 2.4 fusion.45
  130.0 3.9 %fusion.47 = f32[8,1536,128]{2,1,0:T(8,128)} fusion(f32[8,1536,128]{2,1,0:T(8,128)} %get-tuple-element.199, s32[]{:T(128)} %get-tuple-element.196, f32[1536,1536]{0,1:T(8,128)S(1)} %get-tuple-element.182, f32[1536]{0:T(1024)S(1)} %get-tuple-element.181, bf16[1536,1024]{1,0:T(8,128)(2,1)} %get-tuple-element.215, s32[]{:T(128)S(6)} %select_n.22, ...), kind=kOutput, calls=%fused_computation.8.clone.1 | convolution fusion | flops 608894976 | bytes 10629636 | tf_op jit(solution)/shard_map/while/body/eval_jaxpr/dot_general | solution.py:69
  136.7 2.4 fusion.45
  139.2 3.9 %fusion.47 = f32[8,1536,128]{2,1,0:T(8,128)} fusion(f32[8,1536,128]{2,1,0:T(8,128)} %get-tuple-element.199, s32[]{:T(128)} %get-tuple-element.196, f32[1536,1536]{0,1:T(8,128)S(1)} %get-tuple-element.182, f32[1536]{0:T(1024)S(1)} %get-tuple-element.181, bf16[1536,1024]{1,0:T(8,128)(2,1)} %get-tuple-element.215, s32[]{:T(128)S(6)} %select_n.22, ...), kind=kOutput, calls=%fused_computation.8.clone.1 | convolution fusion | flops 608894976 | bytes 10629636 | tf_op jit(solution)/shard_map/while/body/eval_jaxpr/dot_general | solution.py:69
  145.9 2.4 fusion.45
  148.3 3.9 %fusion.47 = f32[8,1536,128]{2,1,0:T(8,128)} fusion(f32[8,1536,128]{2,1,0:T(8,128)} %get-tuple-element.199, s32[]{:T(128)} %get-tuple-element.196, f32[1536,1536]{0,1:T(8,128)S(1)} %get-tuple-element.182, f32[1536]{0:T(1024)S(1)} %get-tuple-element.181, bf16[1536,1024]{1,0:T(8,128)(2,1)} %get-tuple-element.215, s32[]{:T(128)S(6)} %select_n.22, ...), kind=kOutput, calls=%fused_computation.8.clone.1 | convolution fusion | flops 608894976 | bytes 10629636 | tf_op jit(solution)/shard_map/while/body/eval_jaxpr/dot_general | solution.py:69
  155.1 2.4 fusion.45
  157.5 3.9 %fusion.47 = f32[8,1536,128]{2,1,0:T(8,128)} fusion(f32[8,1536,128]{2,1,0:T(8,128)} %get-tuple-element.199, s32[]{:T(128)} %get-tuple-element.196, f32[1536,1536]{0,1:T(8,128)S(1)} %get-tuple-element.182, f32[1536]{0:T(1024)S(1)} %get-tuple-element.181, bf16[1536,1024]{1,0:T(8,128)(2,1)} %get-tuple-element.215, s32[]{:T(128)S(6)} %select_n.22, ...), kind=kOutput, calls=%fused_computation.8.clone.1 | convolution fusion | flops 608894976 | bytes 10629636 | tf_op jit(solution)/shard_map/while/body/eval_jaxpr/dot_general | solution.py:69
  164.3 2.4 fusion.45
  166.7 3.9 %fusion.47 = f32[8,1536,128]{2,1,0:T(8,128)} fusion(f32[8,1536,128]{2,1,0:T(8,128)} %get-tuple-element.199, s32[]{:T(128)} %get-tuple-element.196, f32[1536,1536]{0,1:T(8,128)S(1)} %get-tuple-element.182, f32[1536]{0:T(1024)S(1)} %get-tuple-element.181, bf16[1536,1024]{1,0:T(8,128)(2,1)} %get-tuple-element.215, s32[]{:T(128)S(6)} %select_n.22, ...), kind=kOutput, calls=%fused_computation.8.clone.1 | convolution fusion | flops 608894976 | bytes 10629636 | tf_op jit(solution)/shard_map/while/body/eval_jaxpr/dot_general | solution.py:69
  173.4 2.4 fusion.45
  175.8 3.9 %fusion.47 = f32[8,1536,128]{2,1,0:T(8,128)} fusion(f32[8,1536,128]{2,1,0:T(8,128)} %get-tuple-element.199, s32[]{:T(128)} %get-tuple-element.196, f32[1536,1536]{0,1:T(8,128)S(1)} %get-tuple-element.182, f32[1536]{0:T(1024)S(1)} %get-tuple-element.181, bf16[1536,1024]{1,0:T(8,128)(2,1)} %get-tuple-element.215, s32[]{:T(128)S(6)} %select_n.22, ...), kind=kOutput, calls=%fused_computation.8.clone.1 | convolution fusion | flops 608894976 | bytes 10629636 | tf_op jit(solution)/shard_map/while/body/eval_jaxpr/dot_general | solution.py:69
  182.6 2.4 fusion.45
  185.0 3.9 %fusion.47 = f32[8,1536,128]{2,1,0:T(8,128)} fusion(f32[8,1536,128]{2,1,0:T(8,128)} %get-tuple-element.199, s32[]{:T(128)} %get-tuple-element.196, f32[1536,1536]{0,1:T(8,128)S(1)} %get-tuple-element.182, f32[1536]{0:T(1024)S(1)} %get-tuple-element.181, bf16[1536,1024]{1,0:T(8,128)(2,1)} %get-tuple-element.215, s32[]{:T(128)S(6)} %select_n.22, ...), kind=kOutput, calls=%fused_computation.8.clone.1 | convolution fusion | flops 608894976 | bytes 10629636 | tf_op jit(solution)/shard_map/while/body/eval_jaxpr/dot_general | solution.py:69
  191.5 7.2 %reduce.3 = f32[1536,8]{1,0:T(8,128)S(1)} reduce(f32[1536,1,8]{2,1,0:T(1,128)S(1)} %bitcast.121, f32[]{:T(128)} %broadcast.133), dimensions={1}, to_apply=%bitcast.104.reduce_sub_computation | reduce | bytes 98308
  199.7 5.8 %all-to-all-start.4 = ((f32[8,1,1536]{2,1,0:T(1,128)}), f32[8,1,1536]{2,1,0:T(1,128)S(1)}, u32[]{:S(2)}, u32[]{:S(2)}) async-start(f32[8,1,1536]{2,1,0:T(1,128)} %reshape.160), calls=%async_computation.4 | async-start | bytes 98304 | tf_op jit(solution)/shard_map/all_to_all | solution.py:125
  220.5 7.2 %reduce.1 = f32[1536,8]{1,0:T(8,128)S(1)} reduce(f32[1536,1,8]{2,1,0:T(1,128)S(1)} %bitcast.122, f32[]{:T(128)} %broadcast.133), dimensions={1}, to_apply=%bitcast.106.reduce_sub_computation | reduce | bytes 98308
  228.7 5.7 %all-to-all-start.5 = ((f32[8,1,1536]{2,1,0:T(1,128)}), f32[8,1,1536]{2,1,0:T(1,128)S(1)}, u32[]{:S(2)}, u32[]{:S(2)}) async-start(f32[8,1,1536]{2,1,0:T(1,128)} %reshape.162), calls=%async_computation.5 | async-start | bytes 98304 | tf_op jit(solution)/shard_map/all_to_all | solution.py:126
  238.7 6.6 %all-to-all-start.3 = ((f32[8,1,8,192,128]{4,3,2,1,0:T(8,128)}), f32[8,1,8,192,128]{4,3,2,1,0:T(8,128)}, u32[]{:S(2)}, u32[]{:S(2)}) async-start(f32[8,1,8,192,128]{4,3,2,1,0:T(8,128)} %fusion.21), calls=%async_computation.3 | async-start | bytes 12582912 | tf_op jit(solution)/shard_map/all_to_all | solution.py:16
  250.1 84.7 %all-to-all-done.3 = f32[8,1,8,192,128]{4,3,2,1,0:T(8,128)} async-done(((f32[8,1,8,192,128]{4,3,2,1,0:T(8,128)}), f32[8,1,8,192,128]{4,3,2,1,0:T(8,128)}, u32[]{:S(2)}, u32[]{:S(2)}) %all-to-all-start.3) | async-done | bytes 6291488 | tf_op jit(solution)/shard_map/all_to_all | solution.py:16
  334.8 4.5 %fusion.20 = f32[8,192,128]{2,1,0:T(8,128)S(1)} fusion(f32[8,1,8,192,128]{4,3,2,1,0:T(8,128)} %all-to-all-done.3, f32[8,8,192]{2,1,0:T(8,128)S(1)} %get-tuple-element.101), kind=kLoop, calls=%fused_computation.19 | loop fusion | flops 2949120 | bytes 7127040 | tf_op jit(solution)/shard_map/reduce_sum | solution.py:85
  340.0 11.2 %all_to_all.116 = bf16[2,96,1024]{2,1,0:T(8,128)(2,1)S(1)} all-to-all(bf16[2,96,1024]{2,1,0:T(8,128)(2,1)S(1)} %convert_element_type.32), channel_id=1, replica_groups=mesh['pb'=8,'kv'=8,'ha'=2] {'ha'}, dimensions={0} | all-to-all | bytes 786432 | tf_op jit(solution)/shard_map/all_to_all | solution.py:131
  (107 shorter events, 53.5 us)
Async XLA Ops:
  6.5 64.7 %all-gather.3.cloned.1.call-start = ((), (), s32[]{:S(2)}) async-start(), calls=%async_computation.7 | async-start | bytes 3538944 | tf_op jit(solution)/shard_map/all_gather | solution.py:114
  25.6 15.1 %all-to-all-start.1 = ((bf16[96,2,1024]{2,0,1:T(8,128)(2,1)}), bf16[96,2,1024]{2,0,1:T(8,128)(2,1)S(1)}, u32[]{:S(2)}, u32[]{:S(2)}) async-start(bf16[96,2,1024]{2,0,1:T(8,128)(2,1)} %bitcast.112), calls=%async_computation.1 | async-start | bytes 786432 | tf_op jit(solution)/shard_map/all_to_all | solution.py:111
  29.1 81.9 %all-gather.5.cloned.1.call-start = ((), (), s32[]{:S(2)}) async-start(), calls=%async_computation.8 | async-start | bytes 7077888 | tf_op jit(solution)/shard_map/all_gather | solution.py:31
  199.7 29.0 %all-to-all-start.4 = ((f32[8,1,1536]{2,1,0:T(1,128)}), f32[8,1,1536]{2,1,0:T(1,128)S(1)}, u32[]{:S(2)}, u32[]{:S(2)}) async-start(f32[8,1,1536]{2,1,0:T(1,128)} %reshape.160), calls=%async_computation.4 | async-start | bytes 98304 | tf_op jit(solution)/shard_map/all_to_all | solution.py:125
  228.7 10.0 %all-to-all-start.5 = ((f32[8,1,1536]{2,1,0:T(1,128)}), f32[8,1,1536]{2,1,0:T(1,128)S(1)}, u32[]{:S(2)}, u32[]{:S(2)}) async-start(f32[8,1,1536]{2,1,0:T(1,128)} %reshape.162), calls=%async_computation.5 | async-start | bytes 98304 | tf_op jit(solution)/shard_map/all_to_all | solution.py:126
  238.7 96.0 %all-to-all-start.3 = ((f32[8,1,8,192,128]{4,3,2,1,0:T(8,128)}), f32[8,1,8,192,128]{4,3,2,1,0:T(8,128)}, u32[]{:S(2)}, u32[]{:S(2)}) async-start(f32[8,1,8,192,128]{4,3,2,1,0:T(8,128)} %fusion.21), calls=%async_computation.3 | async-start | bytes 12582912 | tf_op jit(solution)/shard_map/all_to_all | solution.py:16
Sparse Core Ops, SparseCore 0:
  25.0 41.8 all-gather.2
  71.3 39.6 all-gather.4
